TPU v7x, 32 devices: a whole 2x2x4 slice. The times are simulated.
32 devices in a mesh: gx: 4 (over z), gy: 4 (over x, core), gz: 2 (over y).
Axes of the slice: x: 2, y: 2, z: 4, core: 2. Of those that a mesh axis runs over, the one named last changes fastest.
Arguments:
- state: float32 [7, 64, 64, 256], P(None, 'gx', 'gy', 'gz'), may hold values from -1 to 4, as said below
- solver_owner: int32 [4, 2, 8], P('gy', 'gz'), may hold values from 0 to 15, as said below
- phi_prev: float32 [16, 8, 64, 256], P('gx', None, 'gy', 'gz'), may hold values from -1.2 to 1.2
Outputs:
- new_state: float32 [7, 64, 64, 256], P(None, 'gx', 'gy', 'gz')
- density_solver: float32 [16, 8, 64, 256], P('gx', None, 'gy', 'gz')
- residual: float32 [64, 64, 256], P('gx', 'gy', 'gz')
Inputs may be any that keep to these rules, and one draw needn't show every extreme that they name: `state`: field 0 lies in [1, 2], fields 1 to 3 in [-1, 1], field 4 in [2, 4], field 5 in [1, 2], field 6 in [0, 1]. `solver_owner`: entry b of line (j, k) is owner * 4 + slot, the owner being the gx index holding box b in the solver ownership. Codes within a line are distinct, so an owner holds at most 4 boxes of a line, and in every line some owner holds exactly 4.
All inputs are finite; a program needn't handle non-finite values.
Results may differ from a plain program's by a relative error of at most 0.00012.
Values sent between devices are 32-bit elements; how exact they have to be, the bound alone decides.
A program may use at most 64 MiB of HBM per device.

v0:
```python
import jax
import jax.numpy as jnp
from jax import lax
from jax.sharding import PartitionSpec as P

GAMMA = 5.0 / 3.0
DTH = 0.04
FOURPIG = 2.0


def padded_2(cells, sides, width):
    for axis, dim in sides:
        count = lax.axis_size(axis)
        head = lax.slice_in_dim(cells, 0, width, axis=dim)
        tail = lax.slice_in_dim(cells, cells.shape[dim] - width, cells.shape[dim], axis=dim)
        cells = jnp.concatenate(
            [
                lax.ppermute(tail, axis, [(i, (i + 1) % count) for i in range(count)]),
                cells,
                lax.ppermute(head, axis, [((i + 1) % count, i) for i in range(count)]),
            ],
            axis=dim,
        )
    return cells


def wave_speed(q, d):
    dens = jnp.maximum(q[0], 0.25)
    vel = q[d] / dens
    press = (GAMMA - 1.0) * jnp.maximum(q[5], 0.1)
    return jnp.abs(vel) + jnp.sqrt(GAMMA * press / dens)


def physical_flux(v, d):
    dens = jnp.maximum(v[0], 0.25)
    vel = v[d] / dens
    press = (GAMMA - 1.0) * jnp.maximum(v[5], 0.1)
    comps = [v[d]]
    for k in (1, 2, 3):
        term = v[k] * vel
        if k == d:
            term = term + press
        comps.append(term)
    comps.append((v[4] + press) * vel)
    comps.append(v[5] * vel)
    comps.append(v[6] * vel)
    return jnp.stack(comps, 0)


def tendency(padded):
    total = None
    for d in (1, 2, 3):
        line = padded
        for e in (1, 2, 3):
            if e != d:
                line = lax.slice_in_dim(line, 2, line.shape[e] - 2, axis=e)
        count = line.shape[d] - 3
        left_far = lax.slice_in_dim(line, 0, count, axis=d)
        left = lax.slice_in_dim(line, 1, count + 1, axis=d)
        right = lax.slice_in_dim(line, 2, count + 2, axis=d)
        right_far = lax.slice_in_dim(line, 3, count + 3, axis=d)
        edge = 7.0 / 12.0 * (left + right) - 1.0 / 12.0 * (left_far + right_far)
        edge = jnp.clip(edge, jnp.minimum(left, right), jnp.maximum(left, right))
        speed = wave_speed(line, d)
        fastest = jnp.maximum(
            lax.slice_in_dim(speed, 1, count + 1, axis=d - 1),
            lax.slice_in_dim(speed, 2, count + 2, axis=d - 1),
        )
        flux = physical_flux(edge, d) - 0.5 * fastest[None] * (right - left)
        change = lax.slice_in_dim(flux, 1, count, axis=d) - lax.slice_in_dim(
            flux, 0, count - 1, axis=d
        )
        total = change if total is None else total + change
    return -total


def widen(field):
    return padded_2(field, (("gx", 1), ("gy", 2), ("gz", 3)), 2)


def on_device(state, solver_owner, phi_prev):
    fields, cx, cy, cz = state.shape
    slots, half = (phi_prev.shape[0], phi_prev.shape[1])
    codes = solver_owner.reshape(-1)
    position = lax.axis_index("gx")
    first = state + DTH * tendency(widen(state))
    new_state = 0.5 * state + 0.5 * (first + DTH * tendency(widen(first)))
    density = new_state[0]
    boxes = density.reshape(2, half, cy, cz)
    wanted = position * slots + jnp.arange(slots, dtype=jnp.int32)
    piece = lax.all_gather(boxes, "gx", axis=0, tiled=True)
    count = piece.shape[0]
    select = (wanted[:, None] == codes[None, :]).astype(jnp.float32)
    density_solver = jnp.dot(
        select,
        piece.reshape(count, -1),
        precision=lax.Precision.HIGHEST,
        preferred_element_type=jnp.float32,
    ).reshape(slots, half, cy, cz)
    peers = lax.axis_size("gx")
    select = (codes[:, None] == wanted[None, :]).astype(jnp.float32)
    outgoing = jnp.dot(
        select,
        phi_prev.reshape(slots, -1),
        precision=lax.Precision.HIGHEST,
        preferred_element_type=jnp.float32,
    ).reshape(peers, 2, half * cy * cz)
    incoming = lax.all_to_all(outgoing, "gx", split_axis=0, concat_axis=0, tiled=True)
    potential = jnp.sum(incoming, 0).reshape(cx, cy, cz)
    bordered = padded_2(potential, (("gx", 0), ("gy", 1), ("gz", 2)), 1)
    beside_all = bordered[2:, 1:-1, 1:-1] + bordered[:-2, 1:-1, 1:-1]
    beside_all = beside_all + bordered[1:-1, 2:, 1:-1] + bordered[1:-1, :-2, 1:-1]
    beside_all = beside_all + bordered[1:-1, 1:-1, 2:] + bordered[1:-1, 1:-1, :-2]
    laplace = beside_all - 6.0 * potential
    total_mass = lax.psum(jnp.sum(density), ("gx", "gy", "gz"))
    cells_all = cx * cy * cz * lax.axis_size("gx") * lax.axis_size("gy") * lax.axis_size("gz")
    mean = total_mass / cells_all
    residual = FOURPIG * (density - mean) - laplace
    return (new_state, density_solver, residual)


def solution(mesh):
    placed = (P(None, "gx", "gy", "gz"), P("gy", "gz", None), P("gx", None, "gy", "gz"))
    return jax.shard_map(
        on_device,
        mesh=mesh,
        in_specs=placed,
        out_specs=(P(None, "gx", "gy", "gz"), P("gx", None, "gy", "gz"), P("gx", "gy", "gz")),
        check_vma=False,
    )
```

profile of v0, /device:TPU:0, one launch (start us, length us, event | category | flops | bytes accessed | tf_op | source)
XLA Modules:
  0.0 170.2 jit_solution(10727323280041994018)
XLA Ops:
  1.7 3.1 %collective-permute-start = (f32[7,2,16,128]{3,2,1,0:T(8,128)S(1)}, f32[7,2,16,128]{3,2,1,0:T(8,128)S(1)}, u32[]{:S(2)}, u32[]{:S(2)}) collective-permute-start(f32[7,2,16,128]{3,2,1,0:T(8,128)S(1)} %get-tuple-element.49), channel_id=1, source_target_pairs={{0,8},{8,16},{16,24},{24,0},{1,9},{9,17},{17,25},{25,1},{2,10},{10... | collective-permute-start | bytes 344072 | tf_op jit(solution)/shard_map/ppermute | solution.py:18
  4.8 2.1 %collective-permute-start.1 = (f32[7,2,16,128]{3,2,1,0:T(8,128)S(1)}, f32[7,2,16,128]{3,2,1,0:T(8,128)S(1)}, u32[]{:S(2)}, u32[]{:S(2)}) collective-permute-start(f32[7,2,16,128]{3,2,1,0:T(8,128)S(1)} %get-tuple-element.48), channel_id=1, source_target_pairs={{8,0},{16,8},{24,16},{0,24},{9,1},{17,9},{25,17},{1,25},{10,2},{18... | collective-permute-start | bytes 344072 | tf_op jit(solution)/shard_map/ppermute | solution.py:20
  8.9 1.8 %reshape.138 = f32[4,16384,1]{1,0,2:T(4,128)} reshape(f32[4,8,16,128]{3,2,1,0:T(8,128)} %param.5) | data formatting | bytes 524288 | tf_op jit(solution)/shard_map/reshape | solution.py:104
  12.7 1.7 %collective-permute-start.3 = (f32[7,20,2,128]{3,2,1,0:T(2,128)S(1)}, f32[7,20,2,128]{3,2,1,0:T(2,128)S(1)}, u32[]{:S(2)}, u32[]{:S(2)}) collective-permute-start(f32[7,20,2,128]{3,2,1,0:T(2,128)S(1)} %get-tuple-element.40), channel_id=1, source_target_pairs={{2,0},{4,2},{6,4},{0,6},{3,1},{5,3},{7,5},{1,7},{10,8},{12,10},{14... | collective-permute-start | bytes 430088 | tf_op jit(solution)/shard_map/ppermute | solution.py:20
  20.2 1.8 %fusion.145 = (f32[7,20,20,2]{3,2,1,0:T(8,128)}, f32[7,20,20,2]{3,2,1,0:T(8,128)S(1)}) fusion(f32[7,20,20,128]{3,2,1,0:T(8,128)S(1)} %pad_maximum_fusion.2), kind=kLoop, calls=%fused_computation.286 | loop fusion | bytes 89600 | tf_op jit(solution)/shard_map/slice | solution.py:15
  22.0 2.4 %copy.23 = f32[7,20,20,2]{2,3,1,0:T(2,128)S(1)} copy(f32[7,20,20,2]{3,2,1,0:T(8,128)} %get-tuple-element.29) | data formatting | bytes 44800 | tf_op jit(solution)/shard_map/slice | solution.py:15
  28.0 2.7 %multiply_subtract_fusion.3 = f32[7,16,17,128]{3,2,1,0:T(8,128)} fusion(f32[7,16,17,128]{3,2,1,0:T(8,128)} %copy-done.19, f32[16,17,128]{2,1,0:T(8,128)S(1)} %fusion.83, f32[7,20,16,128]{3,2,1,0:T(8,128)S(1)} %get-tuple-element.59, f32[7,20,2,128]{3,2,1,0:T(2,128)S(1)} %collective-permute-done.2, f32[7,20,2,128]{3,2,1,0:T(2,128)S(1)} %collective-permute-done.3), kind=kLoop, calls=%fused_computation.39 | loop fusion | flops 1218560 | bytes 3522560 | tf_op jit(solution)/shard_map/sub | solution.py:69
  31.1 1.9 %copy.24 = f32[7,20,20,2]{3,2,1,0:T(8,128)S(1)} copy(f32[7,20,20,2]{2,3,1,0:T(2,128)} %collective-permute-done.4) | data formatting | bytes 44800 | tf_op jit(solution)/shard_map/ppermute | solution.py:18
  34.3 3.1 %copy.26 = f32[7,20,20,2]{3,2,1,0:T(8,128)} copy(f32[7,20,20,2]{2,3,1,0:T(2,128)} %collective-permute-done.5) | data formatting | bytes 44800 | tf_op jit(solution)/shard_map/ppermute | solution.py:20
  39.3 2.3 %maximum_maximum_fusion = (f32[7,20,20,130]{3,2,1,0:T(8,128)S(1)}, f32[7,20,20,130]{3,2,1,0:T(8,128)S(1)}) fusion(f32[7,20,2,128]{3,2,1,0:T(2,128)S(1)} %collective-permute-done.3, f32[7,20,16,128]{3,2,1,0:T(8,128)S(1)} %get-tuple-element.59, f32[7,20,2,128]{3,2,1,0:T(2,128)S(1)} %collective-permute-done.2, f32[7,20,20,2]{3,2,1,0:T(8,128)S(1)} %copy.24, ...), kind=kLoop, calls=%fused_computation | loop fusion | flops 2184000 | bytes 4390400 | tf_op jit(solution)/shard_map/concatenate | solution.py:16
  47.1 2.7 %collective-permute-start.7 = (f32[7,2,16,128]{3,2,1,0:T(8,128)S(1)}, f32[7,2,16,128]{3,2,1,0:T(8,128)S(1)}, u32[]{:S(2)}, u32[]{:S(2)}) collective-permute-start(f32[7,2,16,128]{3,2,1,0:T(8,128)S(1)} %get-tuple-element.44), channel_id=1, source_target_pairs={{8,0},{16,8},{24,16},{0,24},{9,1},{17,9},{25,17},{1,25},{10,2},{18... | collective-permute-start | bytes 344072 | tf_op jit(solution)/shard_map/ppermute | solution.py:20
  51.3 4.1 %all-to-all-start = ((f32[4,2,16384]{2,1,0:T(2,128)}), f32[4,2,16384]{2,1,0:T(2,128)}, u32[]{:S(2)}, u32[]{:S(2)}) async-start(f32[4,2,16384]{2,1,0:T(2,128)} %fusion.131), calls=%async_computation | async-start | bytes 1048576 | tf_op jit(solution)/shard_map/all_to_all | solution.py:108
  56.3 1.7 %collective-permute-start.9 = (f32[7,20,2,128]{3,2,1,0:T(2,128)S(1)}, f32[7,20,2,128]{3,2,1,0:T(2,128)S(1)}, u32[]{:S(2)}, u32[]{:S(2)}) collective-permute-start(f32[7,20,2,128]{3,2,1,0:T(2,128)S(1)} %get-tuple-element.38), channel_id=1, source_target_pairs={{2,0},{4,2},{6,4},{0,6},{3,1},{5,3},{7,5},{1,7},{10,8},{12,10},{14... | collective-permute-start | bytes 430088 | tf_op jit(solution)/shard_map/ppermute | solution.py:20
  66.4 2.3 %fusion.144 = (f32[7,20,20,2]{3,2,1,0:T(8,128)}, f32[7,20,20,2]{3,2,1,0:T(8,128)}) fusion(f32[7,20,20,128]{3,2,1,0:T(8,128)S(1)} %pad_maximum_fusion.4), kind=kLoop, calls=%fused_computation.285 | loop fusion | bytes 89600 | tf_op jit(solution)/shard_map/slice | solution.py:15
  68.7 3.0 %copy.29 = f32[7,20,20,2]{2,3,1,0:T(2,128)} copy(f32[7,20,20,2]{3,2,1,0:T(8,128)} %get-tuple-element.27) | data formatting | bytes 44800 | tf_op jit(solution)/shard_map/slice | solution.py:15
  73.3 3.0 %copy.31 = f32[7,20,20,2]{2,3,1,0:T(2,128)} copy(f32[7,20,20,2]{3,2,1,0:T(8,128)} %get-tuple-element.28) | data formatting | bytes 44800 | tf_op jit(solution)/shard_map/slice | solution.py:14
  76.8 3.1 %multiply_subtract_fusion.2 = f32[7,16,17,128]{3,2,1,0:T(8,128)} fusion(f32[7,16,17,128]{3,2,1,0:T(8,128)} %copy-done.20, f32[7,20,18,128]{3,2,1,0:T(8,128)} %copy-done, f32[7,20,18,128]{3,2,1,0:T(8,128)S(1)} %get-tuple-element.35, f32[16,17,128]{2,1,0:T(8,128)} %fusion.70), kind=kLoop, calls=%fused_computation.38 | loop fusion | flops 731136 | bytes 4038656 | tf_op jit(solution)/shard_map/sub | solution.py:69
  79.9 1.9 %copy.30 = f32[7,20,20,2]{3,2,1,0:T(8,128)S(1)} copy(f32[7,20,20,2]{2,3,1,0:T(2,128)} %collective-permute-done.10) | data formatting | bytes 44800 | tf_op jit(solution)/shard_map/ppermute | solution.py:18
  83.0 3.1 %copy.32 = f32[7,20,20,2]{3,2,1,0:T(8,128)} copy(f32[7,20,20,2]{2,3,1,0:T(2,128)} %collective-permute-done.11) | data formatting | bytes 44800 | tf_op jit(solution)/shard_map/ppermute | solution.py:20
  86.1 5.3 %maximum_maximum_fusion.1 = (f32[7,20,20,130]{3,2,1,0:T(8,128)S(1)}, f32[7,20,20,130]{3,2,1,0:T(8,128)S(1)}) fusion(f32[7,20,2,128]{3,2,1,0:T(2,128)} %copy-done.17, f32[7,2,16,128]{3,2,1,0:T(8,128)} %copy-done.8, f32[7,16,16,128]{3,2,1,0:T(8,128)S(1)} %fusion.40, f32[7,2,16,128]{3,2,1,0:T(8,128)} %copy-done.5, f32[7,20,2,128]{3,2,1,0:T(2,128)} %copy-done.15, ...), kind=kLoop, calls=%fused_computation.2 | loop fusion | flops 3640000 | bytes 4390400 | tf_op jit(solution)/shard_map/concatenate | solution.py:16
  99.1 2.0 %collective-permute-start.13 = (f32[1,16,128]{2,1,0:T(8,128)S(1)}, f32[1,16,128]{2,1,0:T(8,128)S(1)}, u32[]{:S(2)}, u32[]{:S(2)}) collective-permute-start(f32[1,16,128]{2,1,0:T(8,128)S(1)} %get-tuple-element.55), channel_id=1, source_target_pairs={{0,8},{8,16},{16,24},{24,0},{1,9},{9,17},{17,25},{25,1},{2,10},{10... | collective-permute-start | bytes 24584 | tf_op jit(solution)/shard_map/ppermute | solution.py:18
  101.8 1.9 %collective-permute-start.12 = (f32[1,16,128]{2,1,0:T(8,128)S(1)}, f32[1,16,128]{2,1,0:T(8,128)S(1)}, u32[]{:S(2)}, u32[]{:S(2)}) collective-permute-start(f32[1,16,128]{2,1,0:T(8,128)S(1)} %get-tuple-element.54), channel_id=1, source_target_pairs={{8,0},{16,8},{24,16},{0,24},{9,1},{17,9},{25,17},{1,25},{10,2},{18... | collective-permute-start | bytes 24584 | tf_op jit(solution)/shard_map/ppermute | solution.py:20
  106.0 16.8 %all_gather.3 = f32[8,8,16,128]{3,2,1,0:T(8,128)S(1)} all-gather(f32[2,8,16,128]{3,2,1,0:T(8,128)S(1)} %bitcast.35), channel_id=1, replica_groups=mesh['gx'=4,'gy'=4,'gz'=2] {'gx'}, dimensions={0}, use_global_device_ids=true | all-gather | bytes 655360 | tf_op jit(solution)/shard_map/all_gather | solution.py:91
  125.8 42.1 %psum.7 = f32[]{:T(128)} all-reduce(f32[]{:T(128)} %get-tuple-element.41), channel_id=1, replica_groups=mesh['gx'=4,'gy'=4,'gz'=2] {'gx','gy','gz'}, use_global_device_ids=true, to_apply=%region_1.2 | all-reduce | flops 1 | bytes 8 | tf_op jit(solution)/shard_map/psum | solution.py:115
  (180 shorter events, 52.2 us)
Async XLA Ops:
  0.6 10.2 %copy-start.3 = (f32[7,16,16,128]{3,2,1,0:T(8,128)S(1)}, f32[7,16,16,128]{3,2,1,0:T(8,128)}, u32[]{:S(2)}) copy-start(f32[7,16,16,128]{3,2,1,0:T(8,128)} %param.3) | copy-start | bytes 2752516
  1.7 9.1 %collective-permute-start = (f32[7,2,16,128]{3,2,1,0:T(8,128)S(1)}, f32[7,2,16,128]{3,2,1,0:T(8,128)S(1)}, u32[]{:S(2)}, u32[]{:S(2)}) collective-permute-start(f32[7,2,16,128]{3,2,1,0:T(8,128)S(1)} %get-tuple-element.49), channel_id=1, source_target_pairs={{0,8},{8,16},{16,24},{24,0},{1,9},{9,17},{17,25},{25,1},{2,10},{10... | collective-permute-start | bytes 344072 | tf_op jit(solution)/shard_map/ppermute | solution.py:18
  4.8 7.1 %collective-permute-start.1 = (f32[7,2,16,128]{3,2,1,0:T(8,128)S(1)}, f32[7,2,16,128]{3,2,1,0:T(8,128)S(1)}, u32[]{:S(2)}, u32[]{:S(2)}) collective-permute-start(f32[7,2,16,128]{3,2,1,0:T(8,128)S(1)} %get-tuple-element.48), channel_id=1, source_target_pairs={{8,0},{16,8},{24,16},{0,24},{9,1},{17,9},{25,17},{1,25},{10,2},{18... | collective-permute-start | bytes 344072 | tf_op jit(solution)/shard_map/ppermute | solution.py:20
  12.6 4.6 %collective-permute-start.2 = (f32[7,20,2,128]{3,2,1,0:T(2,128)S(1)}, f32[7,20,2,128]{3,2,1,0:T(2,128)S(1)}, u32[]{:S(2)}, u32[]{:S(2)}) collective-permute-start(f32[7,20,2,128]{3,2,1,0:T(2,128)S(1)} %get-tuple-element.39), channel_id=1, source_target_pairs={{0,2},{2,4},{4,6},{6,0},{1,3},{3,5},{5,7},{7,1},{8,10},{10,12},{12... | collective-permute-start | bytes 430088 | tf_op jit(solution)/shard_map/ppermute | solution.py:18
  12.7 5.1 %collective-permute-start.3 = (f32[7,20,2,128]{3,2,1,0:T(2,128)S(1)}, f32[7,20,2,128]{3,2,1,0:T(2,128)S(1)}, u32[]{:S(2)}, u32[]{:S(2)}) collective-permute-start(f32[7,20,2,128]{3,2,1,0:T(2,128)S(1)} %get-tuple-element.40), channel_id=1, source_target_pairs={{2,0},{4,2},{6,4},{0,6},{3,1},{5,3},{7,5},{1,7},{10,8},{12,10},{14... | collective-permute-start | bytes 430088 | tf_op jit(solution)/shard_map/ppermute | solution.py:20
  24.4 6.7 %collective-permute-start.4 = (f32[7,20,20,2]{2,3,1,0:T(2,128)S(1)}, f32[7,20,20,2]{2,3,1,0:T(2,128)}, u32[]{:S(2)}, u32[]{:S(2)}) collective-permute-start(f32[7,20,20,2]{2,3,1,0:T(2,128)S(1)} %copy.23), channel_id=1, source_target_pairs={{0,1},{1,0},{2,3},{3,2},{4,5},{5,4},{6,7},{7,6},{8,9},{9,8},{10,11... | collective-permute-start | bytes 67208 | tf_op jit(solution)/shard_map/ppermute | solution.py:18
  27.5 6.8 %collective-permute-start.5 = (f32[7,20,20,2]{2,3,1,0:T(2,128)}, f32[7,20,20,2]{2,3,1,0:T(2,128)}, u32[]{:S(2)}, u32[]{:S(2)}) collective-permute-start(f32[7,20,20,2]{2,3,1,0:T(2,128)} %copy.25), channel_id=1, source_target_pairs={{1,0},{0,1},{3,2},{2,3},{5,4},{4,5},{7,6},{6,7},{9,8},{8,9},{11,10... | collective-permute-start | bytes 67208 | tf_op jit(solution)/shard_map/ppermute | solution.py:20
  45.9 9.6 %collective-permute-start.6 = (f32[7,2,16,128]{3,2,1,0:T(8,128)S(1)}, f32[7,2,16,128]{3,2,1,0:T(8,128)S(1)}, u32[]{:S(2)}, u32[]{:S(2)}) collective-permute-start(f32[7,2,16,128]{3,2,1,0:T(8,128)S(1)} %get-tuple-element.43), channel_id=1, source_target_pairs={{0,8},{8,16},{16,24},{24,0},{1,9},{9,17},{17,25},{25,1},{2,10},{10... | collective-permute-start | bytes 344072 | tf_op jit(solution)/shard_map/ppermute | solution.py:18
  47.1 8.4 %collective-permute-start.7 = (f32[7,2,16,128]{3,2,1,0:T(8,128)S(1)}, f32[7,2,16,128]{3,2,1,0:T(8,128)S(1)}, u32[]{:S(2)}, u32[]{:S(2)}) collective-permute-start(f32[7,2,16,128]{3,2,1,0:T(8,128)S(1)} %get-tuple-element.44), channel_id=1, source_target_pairs={{8,0},{16,8},{24,16},{0,24},{9,1},{17,9},{25,17},{1,25},{10,2},{18... | collective-permute-start | bytes 344072 | tf_op jit(solution)/shard_map/ppermute | solution.py:20
  51.3 46.1 %all-to-all-start = ((f32[4,2,16384]{2,1,0:T(2,128)}), f32[4,2,16384]{2,1,0:T(2,128)}, u32[]{:S(2)}, u32[]{:S(2)}) async-start(f32[4,2,16384]{2,1,0:T(2,128)} %fusion.131), calls=%async_computation | async-start | bytes 1048576 | tf_op jit(solution)/shard_map/all_to_all | solution.py:108
  55.4 5.7 %copy-start.5 = (f32[7,2,16,128]{3,2,1,0:T(8,128)}, f32[7,2,16,128]{3,2,1,0:T(8,128)S(1)}, u32[]{:S(2)}) copy-start(f32[7,2,16,128]{3,2,1,0:T(8,128)S(1)} %collective-permute-done.6) | copy-start | bytes 344068
  56.2 4.6 %collective-permute-start.8 = (f32[7,20,2,128]{3,2,1,0:T(2,128)S(1)}, f32[7,20,2,128]{3,2,1,0:T(2,128)S(1)}, u32[]{:S(2)}, u32[]{:S(2)}) collective-permute-start(f32[7,20,2,128]{3,2,1,0:T(2,128)S(1)} %get-tuple-element.37), channel_id=1, source_target_pairs={{0,2},{2,4},{4,6},{6,0},{1,3},{3,5},{5,7},{7,1},{8,10},{10,12},{12... | collective-permute-start | bytes 430088 | tf_op jit(solution)/shard_map/ppermute | solution.py:18
  56.3 4.9 %collective-permute-start.9 = (f32[7,20,2,128]{3,2,1,0:T(2,128)S(1)}, f32[7,20,2,128]{3,2,1,0:T(2,128)S(1)}, u32[]{:S(2)}, u32[]{:S(2)}) collective-permute-start(f32[7,20,2,128]{3,2,1,0:T(2,128)S(1)} %get-tuple-element.38), channel_id=1, source_target_pairs={{2,0},{4,2},{6,4},{0,6},{3,1},{5,3},{7,5},{1,7},{10,8},{12,10},{14... | collective-permute-start | bytes 430088 | tf_op jit(solution)/shard_map/ppermute | solution.py:20
  71.7 8.1 %collective-permute-start.10 = (f32[7,20,20,2]{2,3,1,0:T(2,128)}, f32[7,20,20,2]{2,3,1,0:T(2,128)}, u32[]{:S(2)}, u32[]{:S(2)}) collective-permute-start(f32[7,20,20,2]{2,3,1,0:T(2,128)} %copy.29), channel_id=1, source_target_pairs={{0,1},{1,0},{2,3},{3,2},{4,5},{5,4},{6,7},{7,6},{8,9},{9,8},{10,11... | collective-permute-start | bytes 67208 | tf_op jit(solution)/shard_map/ppermute | solution.py:18
  76.3 6.7 %collective-permute-start.11 = (f32[7,20,20,2]{2,3,1,0:T(2,128)}, f32[7,20,20,2]{2,3,1,0:T(2,128)}, u32[]{:S(2)}, u32[]{:S(2)}) collective-permute-start(f32[7,20,20,2]{2,3,1,0:T(2,128)} %copy.31), channel_id=1, source_target_pairs={{1,0},{0,1},{3,2},{2,3},{5,4},{4,5},{7,6},{6,7},{9,8},{8,9},{11,10... | collective-permute-start | bytes 67208 | tf_op jit(solution)/shard_map/ppermute | solution.py:20
  97.4 72.0 %copy-start.21 = (f32[7,16,16,128]{3,2,1,0:T(8,128)}, f32[7,16,16,128]{3,2,1,0:T(8,128)S(1)}, u32[]{:S(2)}) copy-start(f32[7,16,16,128]{3,2,1,0:T(8,128)S(1)} %fusion.35) | copy-start | bytes 2752516
  99.1 5.5 %collective-permute-start.13 = (f32[1,16,128]{2,1,0:T(8,128)S(1)}, f32[1,16,128]{2,1,0:T(8,128)S(1)}, u32[]{:S(2)}, u32[]{:S(2)}) collective-permute-start(f32[1,16,128]{2,1,0:T(8,128)S(1)} %get-tuple-element.55), channel_id=1, source_target_pairs={{0,8},{8,16},{16,24},{24,0},{1,9},{9,17},{17,25},{25,1},{2,10},{10... | collective-permute-start | bytes 24584 | tf_op jit(solution)/shard_map/ppermute | solution.py:18
  101.8 23.6 %copy-start.24 = (s32[4]{0:T(128)S(1)}, s32[4]{0:T(128)}, u32[]{:S(2)}) copy-start(s32[4]{0:T(128)} %copy-done.23) | copy-start | bytes 52
  101.8 23.6 %copy-start.25 = (s32[1,1,8]{2,1,0:T(1,128)S(1)}, s32[1,1,8]{2,1,0:T(1,128)}, u32[]{:S(2)}) copy-start(s32[1,1,8]{2,1,0:T(1,128)} %param.4) | copy-start | bytes 100
  101.8 3.7 %collective-permute-start.12 = (f32[1,16,128]{2,1,0:T(8,128)S(1)}, f32[1,16,128]{2,1,0:T(8,128)S(1)}, u32[]{:S(2)}, u32[]{:S(2)}) collective-permute-start(f32[1,16,128]{2,1,0:T(8,128)S(1)} %get-tuple-element.54), channel_id=1, source_target_pairs={{8,0},{16,8},{24,16},{0,24},{9,1},{17,9},{25,17},{1,25},{10,2},{18... | collective-permute-start | bytes 24584 | tf_op jit(solution)/shard_map/ppermute | solution.py:20
  105.5 17.7 %collective-permute-start.14 = (f32[18,1,128]{2,1,0:T(1,128)S(1)}, f32[18,1,128]{2,1,0:T(1,128)S(1)}, u32[]{:S(2)}, u32[]{:S(2)}) collective-permute-start(f32[18,1,128]{2,1,0:T(1,128)S(1)} %get-tuple-element.53), channel_id=1, source_target_pairs={{2,0},{4,2},{6,4},{0,6},{3,1},{5,3},{7,5},{1,7},{10,8},{12,10},{14... | collective-permute-start | bytes 27656 | tf_op jit(solution)/shard_map/ppermute | solution.py:20
  105.6 17.5 %collective-permute-start.15 = (f32[18,1,128]{2,1,0:T(1,128)S(1)}, f32[18,1,128]{2,1,0:T(1,128)S(1)}, u32[]{:S(2)}, u32[]{:S(2)}) collective-permute-start(f32[18,1,128]{2,1,0:T(1,128)S(1)} %get-tuple-element.52), channel_id=1, source_target_pairs={{0,2},{2,4},{4,6},{6,0},{1,3},{3,5},{5,7},{7,1},{8,10},{10,12},{12... | collective-permute-start | bytes 27656 | tf_op jit(solution)/shard_map/ppermute | solution.py:18
  123.3 46.0 %collective-permute-start.16 = (f32[18,18,1]{2,1,0:T(8,128)S(1)}, f32[18,18,1]{2,1,0:T(8,128)S(1)}, u32[]{:S(2)}, u32[]{:S(2)}) collective-permute-start(f32[18,18,1]{2,1,0:T(8,128)S(1)} %get-tuple-element.50), channel_id=1, source_target_pairs={{1,0},{0,1},{3,2},{2,3},{5,4},{4,5},{7,6},{6,7},{9,8},{8,9},{11,10... | collective-permute-start | bytes 3896 | tf_op jit(solution)/shard_map/ppermute | solution.py:20
  123.9 45.5 %collective-permute-start.17 = (f32[18,18,1]{2,1,0:T(8,128)S(1)}, f32[18,18,1]{2,1,0:T(8,128)S(1)}, u32[]{:S(2)}, u32[]{:S(2)}) collective-permute-start(f32[18,18,1]{2,1,0:T(8,128)S(1)} %get-tuple-element.51), channel_id=1, source_target_pairs={{0,1},{1,0},{2,3},{3,2},{4,5},{5,4},{6,7},{7,6},{8,9},{9,8},{10,11... | collective-permute-start | bytes 3896 | tf_op jit(solution)/shard_map/ppermute | solution.py:18
  (21 other events, 44.8 us)
where the time goes:
time: 171 us; the launch traced here: 170 us
  blocking collectives  58.9 us (34%)
  local copies, waits for them, and re-layouts  35.4 us (21%)
  other arithmetic  34.9 us (20%)
  starting transfers between devices  27.4 us (16%)
  waiting for transfers between devices  9.63 us (6%)
  between operations  2.12 us (1%)
  matrix products  1.95 us (1%)
    psum x1, blocking collectives, on_device(): total_mass = lax.psum(jnp.sum(density), ('gx', 'gy', 'gz'))  42.1 us
    all_gather x1, blocking collectives, on_device(): piece = lax.all_gather(boxes, 'gx', axis=0, tiled=True)  16.8 us
    ppermute x9, starting transfers between devices, padded_2(): lax.ppermute(head, axis, [((i + 1) % count, i) for i in range(count)])  11.8 us
    ppermute x9, starting transfers between devices, padded_2(): lax.ppermute(tail, axis, [(i, (i + 1) % count) for i in range(count)])  11.4 us
    slice x7, local copies, waits for them, and re-layouts, padded_2(): lax.slice_in_dim(cells, cells.shape[dim] - width, cells.shape[dim], axis=...  9.68 us
    concatenate x6, other arithmetic, padded_2(): jnp.concatenate([lax.ppermute(tail, axis, [(i, (i + 1) % count) for i in...  9.58 us
    sub x6, other arithmetic, tendency(): flux = physical_flux(edge, d) - 0.5 * fastest[None] * (right - left)  9.57 us
    unnamed x64, local copies, waits for them, and re-layouts  7.65 us
  transfers between devices with their start and end apart: 19, of which 11 were waited for; matrix products, arithmetic and copies ran while one was open for 27% of the time, Pallas kernels for 0%

commit v1 on v0

v1 whole, which is shorter than its diff:
```python
import functools

import jax
import jax.numpy as jnp
from jax import lax
from jax.experimental import pallas as pl
from jax.experimental.pallas import tpu as pltpu
from jax.sharding import PartitionSpec as P

GAMMA = 5.0 / 3.0
DTH = 0.04
FOURPIG = 2.0
PAD = 8
AXES = ("gx", "gy", "gz")


def edge_value(a, b, c, d):
    e = 7.0 / 12.0 * (b + c) - 1.0 / 12.0 * (a + d)
    return jnp.minimum(jnp.maximum(e, jnp.minimum(b, c)), jnp.maximum(b, c))


def sound(q0, q5):
    rinv = 1.0 / jnp.maximum(q0, 0.25)
    return rinv, jnp.sqrt((GAMMA * (GAMMA - 1.0)) * jnp.maximum(q5, 0.1) * rinv)


def speed_of(q, d):
    rinv, c = sound(q[0], q[5])
    return jnp.abs(q[d]) * rinv + c


def interface_flux(a, b, c, d, far, direction):
    n = len(b)
    e = [edge_value(a[f], b[f], c[f], d[f]) for f in range(n)]
    vel = e[direction] / jnp.maximum(e[0], 0.25)
    press = (GAMMA - 1.0) * jnp.maximum(e[5], 0.1)
    half = 0.5 * far
    out = [e[direction]]
    for k in (1, 2, 3):
        term = e[k] * vel
        out.append(term + press if k == direction else term)
    out.append((e[4] + press) * vel)
    for k in range(5, n):
        out.append(e[k] * vel)
    return [out[f] - half * (c[f] - b[f]) for f in range(n)]


def lanes_change(q, s):
    n = q[0].shape[1]
    low = [pltpu.roll(v, 1, 1) for v in q]
    high = [pltpu.roll(v, n - 1, 1) for v in q]
    higher = [pltpu.roll(v, n - 2, 1) for v in q]
    flux = interface_flux(low, q, high, higher, jnp.maximum(s, pltpu.roll(s, n - 1, 1)), 3)
    return [v - pltpu.roll(v, 1, 1) for v in flux]


def kernel(
    shape, codes, state, phi, new_state, density_solver, residual,
    Q1, Q2, Qp, Sy1, Sy2, Syp, Ry1, Ry2, Ryp, Pz, Pzp, Rz, Rzp_, T, RC, FL, SN, C, Cp,
    PH, Ps, Pr, NS, Dg, DS, RS, M, Mx, My, Mz, send_sem, recv_sem, local_sem,
):
    sizes, fields, cx, cy, cz, slots, half = shape
    gx, gy, gz = sizes
    me = [lax.axis_index(a) for a in AXES]
    peer = lambda i, k: {AXES[i]: lax.rem(me[i] + k, sizes[i])}
    used = [0]
    sends = []

    def send(src, dst, to):
        i = used[0]
        used[0] += 1
        copy = pltpu.make_async_remote_copy(
            src_ref=src, dst_ref=dst, send_sem=send_sem.at[i], recv_sem=recv_sem.at[i],
            device_id=to, device_id_type=pl.DeviceIdType.MESH,
        )
        copy.start()
        sends.append(copy)
        return copy

    load_state = pltpu.make_async_copy(
        state, Q1.at[:, pl.ds(2, cx), pl.ds(PAD, cy)], local_sem.at[0]
    )
    load_state.start()
    load_phi = pltpu.make_async_copy(phi, PH, local_sem.at[1])
    load_phi.start()

    barrier = pltpu.get_barrier_semaphore()
    for i in range(3):
        for k in range(1, sizes[i]):
            pl.semaphore_signal(
                barrier, inc=1, device_id=peer(i, k), device_id_type=pl.DeviceIdType.MESH
            )

    lane = lax.broadcasted_iota(jnp.int32, (cy, cz), 1)
    row = lax.broadcasted_iota(jnp.int32, (cy, cz), 0)
    group = lane // 8
    low_half = lane % 8 < 4
    inner = slice(PAD, PAD + cy)

    def pack_y(Q, Sy, n):
        flat = Q.reshape(n * (cx + 4) * (cy + 2 * PAD), cz)
        for f in range(n):
            for r, y in enumerate((0, 1, cy - 2, cy - 1)):
                at = (f * (cx + 4) + 2) * (cy + 2 * PAD) + PAD + y
                Sy[f, r] = flat[pl.ds(at, cx, stride=cy + 2 * PAD), :]

    def unpack_y(Q, Ry, n):
        flat = Q.reshape(n * (cx + 4) * (cy + 2 * PAD), cz)
        for f in range(n):
            for r, y in enumerate((-2, -1, cy, cy + 1)):
                at = (f * (cx + 4) + 2) * (cy + 2 * PAD) + PAD + y
                flat[pl.ds(at, cx, stride=cy + 2 * PAD), :] = Ry[f, r]

    def pack_z(Q, Pz, n):
        def step(x, packed):
            return tuple(
                jnp.where(group == x, pltpu.roll(Q[f, x + 2, inner, :], 4 + 8 * x, 1), packed[f])
                for f in range(n)
            )

        packed = lax.fori_loop(0, cx, step, tuple(jnp.zeros((cy, cz), jnp.float32) for _ in range(n)))
        for f in range(n):
            Pz[f] = packed[f]

    def exchange(Q, Sy, Ry, Pz, Rz):
        x = [
            send(Q.at[:, pl.ds(cx, 2), pl.ds(PAD, cy)], Q.at[:, pl.ds(0, 2), pl.ds(PAD, cy)], peer(0, 1)),
            send(Q.at[:, pl.ds(2, 2), pl.ds(PAD, cy)], Q.at[:, pl.ds(cx + 2, 2), pl.ds(PAD, cy)], peer(0, gx - 1)),
        ]
        y = [
            send(Sy.at[:, pl.ds(2, 2)], Ry.at[:, pl.ds(0, 2)], peer(1, 1)),
            send(Sy.at[:, pl.ds(0, 2)], Ry.at[:, pl.ds(2, 2)], peer(1, gy - 1)),
        ]
        z = [send(Pz, Rz.at[0], peer(2, 1))]
        if gz > 2:
            z.append(send(Pz, Rz.at[1], peer(2, gz - 1)))
        return x, y, z

    def from_both(Rz):
        return Rz.at[0], Rz.at[1 if gz > 2 else 0]

    def z_main(Q):
        def step(x, carry):
            q = [Q[f, x + 2, inner, :] for f in range(fields)]
            rinv, c = sound(q[0], q[5])
            RC[0, x] = rinv
            RC[1, x] = c
            change = lanes_change(q, jnp.abs(q[3]) * rinv + c)
            for f in range(fields):
                T[f, x] = change[f]
            return carry

        lax.fori_loop(0, cx, step, 0)

    def finish(Q, Sy, Ry, Pz, Rz, update):
        prev, nxt = from_both(Rz)
        left = [jnp.where(low_half, prev[f], Pz[f]) for f in range(fields)]
        left = lanes_change(left, speed_of(left, 3))
        right = [jnp.where(low_half, Pz[f], nxt[f]) for f in range(fields)]
        right = lanes_change(right, speed_of(right, 3))
        for f in range(fields):
            C[f] = jnp.where(low_half, right[f], left[f])
        unpack_y(Q, Ry, fields)
        b = [Ry[f, 1] for f in range(fields)]
        c = [Sy[f, 0] for f in range(fields)]
        flux = interface_flux(
            [Ry[f, 0] for f in range(fields)], b, c, [Sy[f, 1] for f in range(fields)],
            jnp.maximum(speed_of(b, 2), speed_of(c, 2)), 2,
        )
        for f in range(fields):
            FL[f] = flux[f]
        SN[...] = speed_of([Ry[f, 2] for f in range(fields)], 2)

        def x_flux(x, s):
            rows = [[Q[f, x + k, inner, :] for f in range(fields)] for k in range(1, 5)]
            s_next = speed_of(rows[2], 1)
            return interface_flux(*rows, jnp.maximum(s, s_next), 1), s_next

        def step(x, carry):
            before, s = carry
            after, s_next = x_flux(x, s)
            cells = [[Q[f, x + 2, PAD + k : PAD + k + cy, :] for f in range(fields)] for k in (-1, 0, 1, 2)]
            sy = jnp.abs(cells[1][2]) * RC[0, x] + RC[1, x]
            sy_next = jnp.where(row == cy - 1, SN[pl.ds(x, 1), :], pltpu.roll(sy, cy - 1, 0))
            flux = interface_flux(*cells, jnp.maximum(sy, sy_next), 2)
            outer = (lane < 2) | (lane >= cz - 2)
            for f in range(fields):
                low = jnp.where(row == 0, FL[f, pl.ds(x, 1), :], pltpu.roll(flux[f], 1, 0))
                along_z = jnp.where(outer, pltpu.roll(C[f], cz - 4 - 8 * x, 1), T[f, x])
                total = (after[f] - before[f]) + (flux[f] - low) + along_z
                update(f, x, cells[1][f], total)
            return tuple(after), s_next

        s = speed_of([Q[f, 1, inner, :] for f in range(fields)], 1)
        start, s = x_flux(-1, s)
        lax.fori_loop(0, cx, step, (tuple(start), s))

    load_state.wait()
    pack_y(Q1, Sy1, fields)
    pack_z(Q1, Pz.at[0], fields)
    mass = lax.fori_loop(
        0, cx, lambda x, m: m + Q1[0, x + 2, inner, :], jnp.zeros((cy, cz), jnp.float32)
    )
    M[0] = mass[:8] + mass[8:] if cy == 16 else jnp.broadcast_to(jnp.sum(mass, 0, keepdims=True) / 8, (8, cz))
    pl.semaphore_wait(barrier, gx + gy + gz - 3)
    x1, y1, z1 = exchange(Q1, Sy1, Ry1, Pz.at[0], Rz.at[0])
    masses = [send(M.at[0], Mx.at[k - 1], peer(0, k)) for k in range(1, gx)]

    load_phi.wait()
    boxes = cx // half

    def owned(holder, j):
        slot = codes[0, 0, holder * boxes + j] - me[0] * slots
        mine = (slot >= 0) & (slot < slots)
        return jnp.where(mine, PH[jnp.clip(slot, 0, slots - 1)], 0.0)

    phis = []
    for k in range(1, gx):
        for j in range(boxes):
            Ps[k - 1, j] = owned(lax.rem(me[0] + k, gx), j)
        phis.append(send(Ps.at[k - 1], Pr.at[k - 1], peer(0, k)))

    z_main(Q1)

    for copy in masses:
        copy.wait_recv()
    M[1] = M[0] + sum(Mx[k] for k in range(gx - 1))
    masses = [send(M.at[1], My.at[k - 1], peer(1, k)) for k in range(1, gy)]

    for copy in x1 + y1 + z1:
        copy.wait_recv()

    def to_first(f, x, q, total):
        Q2[f, x + 2, inner, :] = q - DTH * total

    finish(Q1, Sy1, Ry1, Pz.at[0], Rz.at[0], to_first)
    pack_y(Q2, Sy2, fields)
    pack_z(Q2, Pz.at[1], fields)
    x2, y2, z2 = exchange(Q2, Sy2, Ry2, Pz.at[1], Rz.at[1])

    for copy in masses:
        copy.wait_recv()
    M[2] = M[1] + sum(My[k] for k in range(gy - 1))
    masses = [send(M.at[2], Mz.at[k - 1], peer(2, k)) for k in range(1, gz)]

    z_main(Q2)

    for copy in x2 + y2 + z2:
        copy.wait_recv()

    def to_new(f, x, q, total):
        value = 0.5 * Q1[f, x + 2, inner, :] + 0.5 * (q - DTH * total)
        NS[f, x] = value
        if f == 0:
            Dg[me[0] * boxes + x // half, x % half] = value

    finish(Q2, Sy2, Ry2, Pz.at[1], Rz.at[1], to_new)
    mine = Dg.at[pl.ds(me[0] * boxes, boxes)]
    dens = [send(mine, mine, peer(0, k)) for k in range(1, gx)]
    out_state = pltpu.make_async_copy(NS, new_state, local_sem.at[2])
    out_state.start()

    for copy in phis:
        copy.wait_recv()
    for j in range(boxes):
        box = owned(me[0], j)
        for k in range(gx - 1):
            box = box + Pr[k, j]
        Qp[0, 2 + j * half : 2 + (j + 1) * half, inner, :] = box
    pack_y(Qp, Syp, 1)
    pack_z(Qp, Pzp, 1)
    xp, yp, zp = exchange(Qp, Syp, Ryp, Pzp, Rzp_)
    for copy in masses:
        copy.wait_recv()
    total = M[2] + sum(Mz[k] for k in range(gz - 1))
    mean = jnp.sum(total) * (1.0 / (cx * cy * cz * gx * gy * gz))
    for copy in xp + yp + zp:
        copy.wait_recv()
    unpack_y(Qp, Ryp, 1)
    prev, nxt = from_both(Rzp_)
    beside = lambda v: pltpu.roll(v, 1, 1) + pltpu.roll(v, cz - 1, 1)
    Cp[...] = jnp.where(
        low_half, beside(jnp.where(low_half, Pzp[0], nxt[0])), beside(jnp.where(low_half, prev[0], Pzp[0]))
    )

    def poisson(x, carry):
        q = Qp[0, x + 2, inner, :]
        along_z = jnp.where((lane == 0) | (lane == cz - 1), pltpu.roll(Cp[...], cz - 4 - 8 * x, 1), beside(q))
        near = Qp[0, x + 1, inner, :] + Qp[0, x + 3, inner, :]
        near = near + Qp[0, x + 2, PAD - 1 : PAD - 1 + cy, :] + Qp[0, x + 2, PAD + 1 : PAD + 1 + cy, :]
        RS[x] = FOURPIG * (NS[0, x] - mean) - (near + along_z - 6.0 * q)
        return carry

    lax.fori_loop(0, cx, poisson, 0)
    out_residual = pltpu.make_async_copy(RS, residual, local_sem.at[3])
    out_residual.start()

    for copy in dens:
        copy.wait_recv()
    for s in range(slots):
        wanted = me[0] * slots + s
        at = jnp.int32(-1)
        for b in range(gx * boxes):
            at = jnp.where(codes[0, 0, b] == wanted, b, at)
        DS[s] = jnp.where(at >= 0, Dg[jnp.maximum(at, 0)], 0.0)
    out_density = pltpu.make_async_copy(DS, density_solver, local_sem.at[4])
    out_density.start()
    for copy in sends:
        copy.wait_send()
    out_state.wait()
    out_residual.wait()
    out_density.wait()


def on_device(sizes, state, solver_owner, phi_prev):
    fields, cx, cy, cz = state.shape
    slots, half = phi_prev.shape[:2]
    gx, gy, gz = sizes
    boxes = cx // half
    f32 = lambda *s: pltpu.VMEM(s, jnp.float32)
    padded = (cx + 4, cy + 2 * PAD, cz)
    n_send = 3 * (4 + min(gz - 1, 2)) + 3 * (gx - 1) + (gy - 1) + (gz - 1)
    out = lambda *s: jax.ShapeDtypeStruct(s, jnp.float32)
    hbm = pl.BlockSpec(memory_space=pl.ANY)
    return pl.pallas_call(
        functools.partial(kernel, (sizes, fields, cx, cy, cz, slots, half)),
        out_shape=(out(*state.shape), out(*phi_prev.shape), out(cx, cy, cz)),
        in_specs=[pl.BlockSpec(memory_space=pltpu.SMEM), hbm, hbm],
        out_specs=(hbm, hbm, hbm),
        scratch_shapes=[
            f32(fields, *padded), f32(fields, *padded), f32(1, *padded),
            f32(fields, 4, cx, cz), f32(fields, 4, cx, cz), f32(1, 4, cx, cz),
            f32(fields, 4, cx, cz), f32(fields, 4, cx, cz), f32(1, 4, cx, cz),
            f32(2, fields, cy, cz), f32(1, cy, cz), f32(2, 2, fields, cy, cz), f32(2, 1, cy, cz),
            f32(fields, cx, cy, cz), f32(2, cx, cy, cz), f32(fields, cx, cz), f32(cx, cz),
            f32(fields, cy, cz), f32(cy, cz),
            f32(slots, half, cy, cz), f32(gx - 1, boxes, half, cy, cz), f32(gx - 1, boxes, half, cy, cz),
            f32(fields, cx, cy, cz), f32(gx * boxes, half, cy, cz), f32(slots, half, cy, cz), f32(cx, cy, cz),
            f32(3, 8, cz), f32(gx - 1, 8, cz), f32(gy - 1, 8, cz), f32(gz - 1, 8, cz),
            pltpu.SemaphoreType.DMA((n_send,)), pltpu.SemaphoreType.DMA((n_send,)), pltpu.SemaphoreType.DMA((5,)),
        ],
        compiler_params=pltpu.CompilerParams(
            collective_id=0, has_side_effects=True, vmem_limit_bytes=63 * 1024 * 1024
        ),
    )(solver_owner, state, phi_prev)


def solution(mesh):
    sizes = tuple(mesh.shape[a] for a in AXES)
    placed = (P(None, "gx", "gy", "gz"), P("gy", "gz", None), P("gx", None, "gy", "gz"))
    return jax.shard_map(
        functools.partial(on_device, sizes),
        mesh=mesh,
        in_specs=placed,
        out_specs=(P(None, "gx", "gy", "gz"), P("gx", None, "gy", "gz"), P("gx", "gy", "gz")),
        check_vma=False,
    )
```

time: 171 us -> 47.6 us (0.28)
  blocking collectives: 58.9 us -> 0 us
  Pallas kernels: 0 us -> 42.7 us
  other arithmetic: 34.9 us -> 0 us
  local copies, waits for them, and re-layouts: 35.4 us -> 3.88 us
  starting transfers between devices: 27.4 us -> 0 us
  waiting for transfers between devices: 9.63 us -> 0 us
  matrix products: 1.95 us -> 0 us
    pallas_call x0 -> x1, Pallas kernels: none -> 42.7 us  [on_device(): pl.pallas_call(functools.partial(kernel, (sizes, fields, cx, cy, cz, slot...]
    psum x1 -> x0, blocking collectives: 42.1 us -> none  [on_device(): total_mass = lax.psum(jnp.sum(density), ('gx', 'gy', 'gz'))]
    ppermute x18 -> x0, starting transfers between devices: 23.3 us -> none  [the longest x9 11.8 us: padded_2(): lax.ppermute(head, axis, [((i + 1) % count, i) for i in range(count)])]
    all_gather x1 -> x0, blocking collectives: 16.8 us -> none  [on_device(): piece = lax.all_gather(boxes, 'gx', axis=0, tiled=True)]
    slice x12 -> x0, local copies, waits for them, and re-layouts: 15.4 us -> none  [the longest x7 9.68 us: padded_2(): lax.slice_in_dim(cells, cells.shape[dim] - width, cells.shape[dim], axis=...]
    sub x7 -> x0, other arithmetic: 10.4 us -> none  [the longest x6 9.57 us: tendency(): flux = physical_flux(edge, d) - 0.5 * fastest[None] * (right - left)]
    ppermute x4 -> x0, local copies, waits for them, and re-layouts: 9.92 us -> none  [the longest x2 6.18 us: padded_2(): lax.ppermute(head, axis, [((i + 1) % count, i) for i in range(count)])]
    ppermute x18 -> x0, waiting for transfers between devices: 9.63 us -> none  [the longest x9 5.04 us: padded_2(): lax.ppermute(head, axis, [((i + 1) % count, i) for i in range(count)])]
  transfers between devices with their start and end apart: 19 -> 0, of which waited for: 11 -> 0; matrix products, arithmetic and copies ran while one was open for 27% -> 0% of each run, Pallas kernels for 0% -> 0%
where the time goes in v1:
time: 47.6 us; the launch traced here: 47.2 us
  Pallas kernels  42.7 us (90%)
  local copies, waits for them, and re-layouts  3.88 us (8%)
  between operations  0.65 us (1%)
    pallas_call x1, Pallas kernels, on_device(): pl.pallas_call(functools.partial(kernel, (sizes, fields, cx, cy, cz, slot...  42.7 us
    unnamed x7, local copies, waits for them, and re-layouts  3.88 us

profile of v1, /device:TPU:0, one launch (start us, length us, event | category | flops | bytes accessed | tf_op | source)
XLA Modules:
  0.0 47.2 jit_solution(9360432904208078759)
XLA Ops:
  0.6 42.7 %shard_map.58 = (f32[7,16,16,128]{3,2,1,0:T(8,128)}, f32[4,8,16,128]{3,2,1,0:T(8,128)}, f32[16,16,128]{2,1,0:T(8,128)}) custom-call(s32[1,1,8]{2,1,0:T(1,128)} %codes.1, f32[7,16,16,128]{3,2,1,0:T(8,128)} %state.1, f32[4,8,16,128]{3,2,1,0:T(8,128)} %phi.1), custom_call_target="tpu_custom_call" | custom-call | tf_op jit(solution)/shard_map/pallas_call | solution.py:325
  43.4 0.0 copy-start
  43.4 2.2 %copy.9 = f32[7,16,16,128]{3,2,1,0:T(8,128)} copy(f32[7,16,16,128]{3,2,1,0:T(8,128)} %get-tuple-element.6) | data formatting | bytes 1835008
  45.6 0.0 copy-done
  45.6 0.0 copy-start.1
  45.6 0.7 %copy.10 = f32[4,8,16,128]{3,2,1,0:T(8,128)} copy(f32[4,8,16,128]{3,2,1,0:T(8,128)S(1)} %copy-done) | data formatting | bytes 524288
  46.3 0.3 copy-done.1
  46.6 0.7 %copy.11 = f32[16,16,128]{2,1,0:T(8,128)} copy(f32[16,16,128]{2,1,0:T(8,128)S(1)} %copy-done.1) | data formatting | bytes 262144
Async XLA Ops:
  43.4 2.2 %copy-start = (f32[4,8,16,128]{3,2,1,0:T(8,128)S(1)}, f32[4,8,16,128]{3,2,1,0:T(8,128)}, u32[]{:S(2)}) copy-start(f32[4,8,16,128]{3,2,1,0:T(8,128)} %get-tuple-element.7) | copy-start | bytes 786436
  45.6 1.0 %copy-start.1 = (f32[16,16,128]{2,1,0:T(8,128)S(1)}, f32[16,16,128]{2,1,0:T(8,128)}, u32[]{:S(2)}) copy-start(f32[16,16,128]{2,1,0:T(8,128)} %get-tuple-element.8) | copy-start | bytes 393220

commit v2 on v1

--- a/solution.py
+++ b/solution.py
@@ -57,7 +57,7 @@
 def kernel(
     shape, codes, state, phi, new_state, density_solver, residual,
     Q1, Q2, Qp, Sy1, Sy2, Syp, Ry1, Ry2, Ryp, Pz, Pzp, Rz, Rzp_, T, RC, FL, SN, C, Cp,
-    PH, Ps, Pr, NS, Dg, DS, RS, M, Mx, My, Mz, send_sem, recv_sem, local_sem,
+    PH, Ps, Pr, Pf, NS, Dg, DS, RS, M, Mx, My, Mz, send_sem, recv_sem, local_sem,
 ):
     sizes, fields, cx, cy, cz, slots, half = shape
     gx, gy, gz = sizes
@@ -76,6 +76,25 @@
         copy.start()
         sends.append(copy)
         return copy
+
+    def channel():
+        used[0] += 1
+        return used[0] - 1
+
+    def copy_on(i, src, dst, to):
+        return pltpu.make_async_remote_copy(
+            src_ref=src, dst_ref=dst, send_sem=send_sem.at[i], recv_sem=recv_sem.at[i],
+            device_id=to, device_id_type=pl.DeviceIdType.MESH,
+        )
+
+    some_sends = []
+
+    def send_if(i, cond, src, dst, to):
+        pl.when(cond)(lambda: copy_on(i, src, dst, to).start())
+        some_sends.append((cond, i, src))
+
+    def wait_if(i, cond, dst):
+        pl.when(cond)(lambda: copy_on(i, dst, dst, peer(0, 1)).wait_recv())
 
     load_state = pltpu.make_async_copy(
         state, Q1.at[:, pl.ds(2, cx), pl.ds(PAD, cy)], local_sem.at[0]
@@ -150,7 +169,7 @@
                 T[f, x] = change[f]
             return carry
 
-        lax.fori_loop(0, cx, step, 0)
+        lax.fori_loop(0, cx, step, 0, unroll=2)
 
     def finish(Q, Sy, Ry, Pz, Rz, update):
         prev, nxt = from_both(Rz)
@@ -208,24 +227,44 @@
 
     load_phi.wait()
     boxes = cx // half
-
-    def owned(holder, j):
-        slot = codes[0, 0, holder * boxes + j] - me[0] * slots
+    here = me[0]
+
+    def owned(slots_ref, owner, holder, j):
+        slot = codes[0, 0, holder * boxes + j] - owner * slots
         mine = (slot >= 0) & (slot < slots)
-        return jnp.where(mine, PH[jnp.clip(slot, 0, slots - 1)], 0.0)
-
-    phis = []
-    for k in range(1, gx):
+        return jnp.where(mine, slots_ref[jnp.clip(slot, 0, slots - 1)], 0.0)
+
+    steps = [d for k in range(1, gx - 1) for d in (k, -k)]
+    direct = {d: channel() for d in steps}
+    hand = [channel(), channel()]
+    second, last = 1, gx - 2
+    send_if(hand[0], here == 0, PH, Pf.at[0], {"gx": second})
+    send_if(hand[1], here == gx - 1, PH, Pf.at[1], {"gx": last})
+    for p in range(gx):
         for j in range(boxes):
-            Ps[k - 1, j] = owned(lax.rem(me[0] + k, gx), j)
-        phis.append(send(Ps.at[k - 1], Pr.at[k - 1], peer(0, k)))
+            Ps[p, j] = owned(PH, here, p, j)
+    inside = (here >= 1) & (here <= gx - 2)
+    for d in steps:
+        p = here + d
+        now = inside & (p >= 0) & (p < gx) & ~((here == second) & (p > second)) & ~((here == last) & (p < last))
+        at = jnp.clip(p, 0, gx - 1)
+        send_if(direct[d], now, Ps.at[at], Pr.at[steps.index(d)], {"gx": at})
+
+    def pass_on():
+        for i, (via, owner) in enumerate(((second, 0), (last, gx - 1))):
+            cond = here == via
+            wait_if(hand[i], cond, Pf.at[i])
+            targets = range(gx - 1, via, -1) if i == 0 else range(via)
+            for p in targets:
+
+                @pl.when(cond)
+                def _():
+                    for j in range(boxes):
+                        Ps[p, j] = Ps[p, j] + owned(Pf.at[i], owner, p, j)
+
+                send_if(direct[p - via], cond, Ps.at[p], Pr.at[steps.index(p - via)], {"gx": p})
 
     z_main(Q1)
-
-    for copy in masses:
-        copy.wait_recv()
-    M[1] = M[0] + sum(Mx[k] for k in range(gx - 1))
-    masses = [send(M.at[1], My.at[k - 1], peer(1, k)) for k in range(1, gy)]
 
     for copy in x1 + y1 + z1:
         copy.wait_recv()
@@ -240,10 +279,16 @@
 
     for copy in masses:
         copy.wait_recv()
+    M[1] = M[0] + sum(Mx[k] for k in range(gx - 1))
+    masses = [send(M.at[1], My.at[k - 1], peer(1, k)) for k in range(1, gy)]
+
+    pass_on()
+    z_main(Q2)
+
+    for copy in masses:
+        copy.wait_recv()
     M[2] = M[1] + sum(My[k] for k in range(gy - 1))
     masses = [send(M.at[2], Mz.at[k - 1], peer(2, k)) for k in range(1, gz)]
-
-    z_main(Q2)
 
     for copy in x2 + y2 + z2:
         copy.wait_recv()
@@ -254,22 +299,56 @@
         if f == 0:
             Dg[me[0] * boxes + x // half, x % half] = value
 
+    block = lambda i: Dg.at[pl.ds(i * boxes, boxes)]
+    spread = {d: channel() for k in range(1, gx) for d in (k, -k)}
+
+    def send_density():
+        for d in sorted(spread, key=lambda d: -abs(d)):
+            if abs(d) < 3:
+                to = here + d
+                send_if(spread[d], (to >= 0) & (to < gx), block(here), block(here), {"gx": to})
+
+    def relay_density():
+        for d in sorted(spread, key=abs):
+            if abs(d) >= 3:
+                one = 1 if d > 0 else -1
+                source, to = here - (d - one), here + one
+                cond = (source >= 0) & (source < gx) & (to >= 0) & (to < gx)
+                wait_if(spread[d - one], cond, block(source))
+                send_if(spread[d], cond, block(source), block(source), {"gx": to})
+
+    def wait_density():
+        for d in spread:
+            source, beyond = here - d, here + (1 if d > 0 else -1)
+            relayed = (abs(d) >= 2) & (beyond >= 0) & (beyond < gx)
+            wait_if(spread[d], (source >= 0) & (source < gx) & ~relayed, block(source))
+
     finish(Q2, Sy2, Ry2, Pz.at[1], Rz.at[1], to_new)
-    mine = Dg.at[pl.ds(me[0] * boxes, boxes)]
-    dens = [send(mine, mine, peer(0, k)) for k in range(1, gx)]
+    send_density()
     out_state = pltpu.make_async_copy(NS, new_state, local_sem.at[2])
     out_state.start()
-
-    for copy in phis:
-        copy.wait_recv()
     for j in range(boxes):
-        box = owned(me[0], j)
-        for k in range(gx - 1):
-            box = box + Pr[k, j]
-        Qp[0, 2 + j * half : 2 + (j + 1) * half, inner, :] = box
+        Qp[0, 2 + j * half : 2 + (j + 1) * half, inner, :] = owned(PH, here, here, j)
+
+    def add_potential(cond, get):
+        @pl.when(cond)
+        def _():
+            for j in range(boxes):
+                at = slice(2 + j * half, 2 + (j + 1) * half)
+                Qp[0, at, inner, :] = Qp[0, at, inner, :] + get(j)
+
+    add_potential(here == second, lambda j: owned(Pf.at[0], 0, here, j))
+    add_potential(here == last, lambda j: owned(Pf.at[1], gx - 1, here, j))
+    for d in steps:
+        source = here - d
+        cond = (source >= 1) & (source <= gx - 2) & (here >= 0)
+        wait_if(direct[d], cond, Pr.at[steps.index(d)])
+        add_potential(cond, lambda j: Pr[steps.index(d), j])
     pack_y(Qp, Syp, 1)
     pack_z(Qp, Pzp, 1)
     xp, yp, zp = exchange(Qp, Syp, Ryp, Pzp, Rzp_)
+    relay_density()
+
     for copy in masses:
         copy.wait_recv()
     total = M[2] + sum(Mz[k] for k in range(gz - 1))
@@ -295,8 +374,7 @@
     out_residual = pltpu.make_async_copy(RS, residual, local_sem.at[3])
     out_residual.start()
 
-    for copy in dens:
-        copy.wait_recv()
+    wait_density()
     for s in range(slots):
         wanted = me[0] * slots + s
         at = jnp.int32(-1)
@@ -307,6 +385,8 @@
     out_density.start()
     for copy in sends:
         copy.wait_send()
+    for cond, i, src in some_sends:
+        pl.when(cond)(lambda: copy_on(i, src, src, peer(0, 1)).wait_send())
     out_state.wait()
     out_residual.wait()
     out_density.wait()
@@ -319,7 +399,7 @@
     boxes = cx // half
     f32 = lambda *s: pltpu.VMEM(s, jnp.float32)
     padded = (cx + 4, cy + 2 * PAD, cz)
-    n_send = 3 * (4 + min(gz - 1, 2)) + 3 * (gx - 1) + (gy - 1) + (gz - 1)
+    n_send = 3 * (4 + min(gz - 1, 2)) + (gx + gy + gz - 3) + (2 * gx - 4) + 2 + (2 * gx - 2)
     out = lambda *s: jax.ShapeDtypeStruct(s, jnp.float32)
     hbm = pl.BlockSpec(memory_space=pl.ANY)
     return pl.pallas_call(
@@ -334,7 +414,7 @@
             f32(2, fields, cy, cz), f32(1, cy, cz), f32(2, 2, fields, cy, cz), f32(2, 1, cy, cz),
             f32(fields, cx, cy, cz), f32(2, cx, cy, cz), f32(fields, cx, cz), f32(cx, cz),
             f32(fields, cy, cz), f32(cy, cz),
-            f32(slots, half, cy, cz), f32(gx - 1, boxes, half, cy, cz), f32(gx - 1, boxes, half, cy, cz),
+            f32(slots, half, cy, cz), f32(gx, boxes, half, cy, cz), f32(2 * gx - 4, boxes, half, cy, cz), f32(2, slots, half, cy, cz),
             f32(fields, cx, cy, cz), f32(gx * boxes, half, cy, cz), f32(slots, half, cy, cz), f32(cx, cy, cz),
             f32(3, 8, cz), f32(gx - 1, 8, cz), f32(gy - 1, 8, cz), f32(gz - 1, 8, cz),
             pltpu.SemaphoreType.DMA((n_send,)), pltpu.SemaphoreType.DMA((n_send,)), pltpu.SemaphoreType.DMA((5,)),

time: 47.6 us -> 44.2 us (0.929)
  Pallas kernels: 42.7 us -> 39.5 us
    pallas_call x1, Pallas kernels: 42.7 us -> 39.5 us  [on_device(): pl.pallas_call(functools.partial(kernel, (sizes, fields, cx, cy, cz, slot...]
where the time goes in v2:
time: 44.2 us; the launch traced here: 44 us
  Pallas kernels  39.5 us (89%)
  local copies, waits for them, and re-layouts  3.88 us (9%)
  between operations  0.65 us (1%)
    pallas_call x1, Pallas kernels, on_device(): pl.pallas_call(functools.partial(kernel, (sizes, fields, cx, cy, cz, slot...  39.5 us
    unnamed x7, local copies, waits for them, and re-layouts  3.88 us

profile of v2, /device:TPU:0, one launch (start us, length us, event | category | flops | bytes accessed | tf_op | source)
XLA Modules:
  0.0 44.0 jit_solution(14160369672612807845)
XLA Ops:
  0.6 39.5 %shard_map.58 = (f32[7,16,16,128]{3,2,1,0:T(8,128)}, f32[4,8,16,128]{3,2,1,0:T(8,128)}, f32[16,16,128]{2,1,0:T(8,128)}) custom-call(s32[1,1,8]{2,1,0:T(1,128)} %codes.1, f32[7,16,16,128]{3,2,1,0:T(8,128)} %state.1, f32[4,8,16,128]{3,2,1,0:T(8,128)} %phi.1), custom_call_target="tpu_custom_call" | custom-call | tf_op jit(solution)/shard_map/pallas_call | solution.py:405
  40.1 0.0 copy-start
  40.2 2.2 %copy.9 = f32[7,16,16,128]{3,2,1,0:T(8,128)} copy(f32[7,16,16,128]{3,2,1,0:T(8,128)} %get-tuple-element.6) | data formatting | bytes 1835008
  42.4 0.0 copy-done
  42.4 0.0 copy-start.1
  42.4 0.7 %copy.10 = f32[4,8,16,128]{3,2,1,0:T(8,128)} copy(f32[4,8,16,128]{3,2,1,0:T(8,128)S(1)} %copy-done) | data formatting | bytes 524288
  43.1 0.3 copy-done.1
  43.4 0.7 %copy.11 = f32[16,16,128]{2,1,0:T(8,128)} copy(f32[16,16,128]{2,1,0:T(8,128)S(1)} %copy-done.1) | data formatting | bytes 262144
Async XLA Ops:
  40.1 2.2 %copy-start = (f32[4,8,16,128]{3,2,1,0:T(8,128)S(1)}, f32[4,8,16,128]{3,2,1,0:T(8,128)}, u32[]{:S(2)}) copy-start(f32[4,8,16,128]{3,2,1,0:T(8,128)} %get-tuple-element.7) | copy-start | bytes 786436
  42.4 1.0 %copy-start.1 = (f32[16,16,128]{2,1,0:T(8,128)S(1)}, f32[16,16,128]{2,1,0:T(8,128)}, u32[]{:S(2)}) copy-start(f32[16,16,128]{2,1,0:T(8,128)} %get-tuple-element.8) | copy-start | bytes 393220

commit v3 on v2

--- a/solution.py
+++ b/solution.py
@@ -55,9 +55,9 @@
 
 
 def kernel(
-    shape, codes, state, phi, new_state, density_solver, residual,
+    shape, codes, state, phi, NS, DS, RS,
     Q1, Q2, Qp, Sy1, Sy2, Syp, Ry1, Ry2, Ryp, Pz, Pzp, Rz, Rzp_, T, RC, FL, SN, C, Cp,
-    PH, Ps, Pr, Pf, NS, Dg, DS, RS, M, Mx, My, Mz, send_sem, recv_sem, local_sem,
+    PH, Ps, Pr, Pf, Dg, M, Mx, My, Mz, send_sem, recv_sem, local_sem,
 ):
     sizes, fields, cx, cy, cz, slots, half = shape
     gx, gy, gz = sizes
@@ -325,8 +325,6 @@
 
     finish(Q2, Sy2, Ry2, Pz.at[1], Rz.at[1], to_new)
     send_density()
-    out_state = pltpu.make_async_copy(NS, new_state, local_sem.at[2])
-    out_state.start()
     for j in range(boxes):
         Qp[0, 2 + j * half : 2 + (j + 1) * half, inner, :] = owned(PH, here, here, j)
 
@@ -371,8 +369,6 @@
         return carry
 
     lax.fori_loop(0, cx, poisson, 0)
-    out_residual = pltpu.make_async_copy(RS, residual, local_sem.at[3])
-    out_residual.start()
 
     wait_density()
     for s in range(slots):
@@ -381,15 +377,20 @@
         for b in range(gx * boxes):
             at = jnp.where(codes[0, 0, b] == wanted, b, at)
         DS[s] = jnp.where(at >= 0, Dg[jnp.maximum(at, 0)], 0.0)
-    out_density = pltpu.make_async_copy(DS, density_solver, local_sem.at[4])
-    out_density.start()
     for copy in sends:
         copy.wait_send()
     for cond, i, src in some_sends:
         pl.when(cond)(lambda: copy_on(i, src, src, peer(0, 1)).wait_send())
-    out_state.wait()
-    out_residual.wait()
-    out_density.wait()
+
+
+def write_out(*refs):
+    n = len(refs) // 2
+    sem = refs[-1]
+    copies = [pltpu.make_async_copy(refs[i], refs[n + i], sem.at[i]) for i in range(n)]
+    for copy in copies:
+        copy.start()
+    for copy in copies:
+        copy.wait()
 
 
 def on_device(sizes, state, solver_owner, phi_prev):
@@ -402,11 +403,12 @@
     n_send = 3 * (4 + min(gz - 1, 2)) + (gx + gy + gz - 3) + (2 * gx - 4) + 2 + (2 * gx - 2)
     out = lambda *s: jax.ShapeDtypeStruct(s, jnp.float32)
     hbm = pl.BlockSpec(memory_space=pl.ANY)
-    return pl.pallas_call(
+    vmem = pl.BlockSpec(memory_space=pltpu.VMEM)
+    results = pl.pallas_call(
         functools.partial(kernel, (sizes, fields, cx, cy, cz, slots, half)),
         out_shape=(out(*state.shape), out(*phi_prev.shape), out(cx, cy, cz)),
-        in_specs=[pl.BlockSpec(memory_space=pltpu.SMEM), hbm, hbm],
-        out_specs=(hbm, hbm, hbm),
+        in_specs=[pl.BlockSpec(memory_space=pltpu.SMEM)] + [pl.BlockSpec(memory_space=pltpu.HBM)] * 2,
+        out_specs=(vmem, vmem, vmem),
         scratch_shapes=[
             f32(fields, *padded), f32(fields, *padded), f32(1, *padded),
             f32(fields, 4, cx, cz), f32(fields, 4, cx, cz), f32(1, 4, cx, cz),
@@ -415,14 +417,22 @@
             f32(fields, cx, cy, cz), f32(2, cx, cy, cz), f32(fields, cx, cz), f32(cx, cz),
             f32(fields, cy, cz), f32(cy, cz),
             f32(slots, half, cy, cz), f32(gx, boxes, half, cy, cz), f32(2 * gx - 4, boxes, half, cy, cz), f32(2, slots, half, cy, cz),
-            f32(fields, cx, cy, cz), f32(gx * boxes, half, cy, cz), f32(slots, half, cy, cz), f32(cx, cy, cz),
+            f32(gx * boxes, half, cy, cz),
             f32(3, 8, cz), f32(gx - 1, 8, cz), f32(gy - 1, 8, cz), f32(gz - 1, 8, cz),
-            pltpu.SemaphoreType.DMA((n_send,)), pltpu.SemaphoreType.DMA((n_send,)), pltpu.SemaphoreType.DMA((5,)),
+            pltpu.SemaphoreType.DMA((n_send,)), pltpu.SemaphoreType.DMA((n_send,)), pltpu.SemaphoreType.DMA((2,)),
         ],
         compiler_params=pltpu.CompilerParams(
-            collective_id=0, has_side_effects=True, vmem_limit_bytes=63 * 1024 * 1024
+            collective_id=0, has_side_effects=True, vmem_limit_bytes=48 * 1024 * 1024
         ),
     )(solver_owner, state, phi_prev)
+    return pl.pallas_call(
+        write_out,
+        out_shape=tuple(out(*r.shape) for r in results),
+        in_specs=[hbm] * 3,
+        out_specs=(pl.BlockSpec(memory_space=pltpu.HBM),) * 3,
+        scratch_shapes=[pltpu.SemaphoreType.DMA((3,))],
+        compiler_params=pltpu.CompilerParams(vmem_limit_bytes=16 * 1024 * 1024),
+    )(*results)
 
 
 def solution(mesh):

time: 44.2 us -> 41.8 us (0.946)
  Pallas kernels: 39.5 us -> 38.2 us
  local copies, waits for them, and re-layouts: 3.88 us -> 2.78 us
    pallas_call x1, Pallas kernels: 39.5 us -> 37.1 us  [on_device(): pl.pallas_call(functools.partial(kernel, (sizes, fields, cx, cy, cz, slot...]
    unnamed x7 -> x6, local copies, waits for them, and re-layouts: 3.88 us -> 2.78 us
    pallas_call x0 -> x1, Pallas kernels: none -> 1.07 us  [on_device(): pl.pallas_call(write_out, out_shape=tuple((out(*r.shape) for r in results...]
where the time goes in v3:
time: 41.8 us; the launch traced here: 41.6 us
  Pallas kernels  38.2 us (91%)
  local copies, waits for them, and re-layouts  2.78 us (7%)
  between operations  0.65 us (2%)
    pallas_call x1, Pallas kernels, on_device(): pl.pallas_call(functools.partial(kernel, (sizes, fields, cx, cy, cz, slot...  37.1 us
    unnamed x6, local copies, waits for them, and re-layouts  2.78 us
    pallas_call x1, Pallas kernels, on_device(): pl.pallas_call(write_out, out_shape=tuple((out(*r.shape) for r in results...  1.07 us

profile of v3, /device:TPU:0, one launch (start us, length us, event | category | flops | bytes accessed | tf_op | source)
XLA Modules:
  0.0 41.6 jit_solution(5748923172852338140)
XLA Ops:
  0.6 0.0 copy-start
  0.6 1.2 %copy-done = f32[7,16,16,128]{3,2,1,0:T(8,128)S(1)} copy-done((f32[7,16,16,128]{3,2,1,0:T(8,128)S(1)}, f32[7,16,16,128]{3,2,1,0:T(8,128)}, u32[]{:S(2)}) %copy-start) | copy-done | bytes 917528
  1.8 0.0 copy-start.1
  1.8 0.9 %copy-done.1 = f32[4,8,16,128]{3,2,1,0:T(8,128)S(1)} copy-done((f32[4,8,16,128]{3,2,1,0:T(8,128)S(1)}, f32[4,8,16,128]{3,2,1,0:T(8,128)}, u32[]{:S(2)}) %copy-start.1) | copy-done | bytes 262168
  2.8 0.0 copy-start.2
  2.8 0.7 %copy-done.2 = s32[1,1,8]{2,1,0:T(1,128)S(1)} copy-done((s32[1,1,8]{2,1,0:T(1,128)S(1)}, s32[1,1,8]{2,1,0:T(1,128)}, u32[]{:S(2)}) %copy-start.2) | copy-done | bytes 56
  3.4 37.1 %shard_map.58 = (f32[7,16,16,128]{3,2,1,0:T(8,128)S(1)}, f32[4,8,16,128]{3,2,1,0:T(8,128)S(1)}, f32[16,16,128]{2,1,0:T(8,128)S(1)}) custom-call(s32[1,1,8]{2,1,0:T(1,128)S(1)} %copy-done.2, f32[7,16,16,128]{3,2,1,0:T(8,128)S(1)} %copy-done, f32[4,8,16,128]{3,2,1,0:T(8,128)S(1)} %copy-done.1), custom_call_target="tpu_custom_call" | custom-call | tf_op jit(solution)/shard_map/pallas_call | solution.py:407
  40.5 1.1 %shard_map.59 = (f32[7,16,16,128]{3,2,1,0:T(8,128)}, f32[4,8,16,128]{3,2,1,0:T(8,128)}, f32[16,16,128]{2,1,0:T(8,128)}) custom-call(f32[7,16,16,128]{3,2,1,0:T(8,128)S(1)} %get-tuple-element.6.refs_0_, f32[4,8,16,128]{3,2,1,0:T(8,128)S(1)} %get-tuple-element.7.refs_1_, f32[16,16,128]{2,1,0:T(8,128)S(1)} %get-tuple-element.8.refs_2_), custom_call_target="tpu_custom_call" | custom-call | tf_op jit(solution)/shard_map/pallas_call | solution.py:428
Async XLA Ops:
  0.6 1.2 %copy-start = (f32[7,16,16,128]{3,2,1,0:T(8,128)S(1)}, f32[7,16,16,128]{3,2,1,0:T(8,128)}, u32[]{:S(2)}) copy-start(f32[7,16,16,128]{3,2,1,0:T(8,128)} %state.1) | copy-start | bytes 2752516
  1.8 0.9 %copy-start.1 = (f32[4,8,16,128]{3,2,1,0:T(8,128)S(1)}, f32[4,8,16,128]{3,2,1,0:T(8,128)}, u32[]{:S(2)}) copy-start(f32[4,8,16,128]{3,2,1,0:T(8,128)} %phi.1) | copy-start | bytes 786436
  2.8 0.7 %copy-start.2 = (s32[1,1,8]{2,1,0:T(1,128)S(1)}, s32[1,1,8]{2,1,0:T(1,128)}, u32[]{:S(2)}) copy-start(s32[1,1,8]{2,1,0:T(1,128)} %codes.1) | copy-start | bytes 100
